TPU v7x, 32 devices: a whole 2x2x4 slice. The times are simulated.
32 devices in a mesh: rows: 16 (over z, y, x), rhs: 2 (over core).
Axes of the slice: x: 2, y: 2, z: 4, core: 2. Of those that a mesh axis runs over, the one named last changes fastest.
Arguments:
- rhs: float32 [2, 8192, 4096], P(None, 'rows', 'rhs'), may hold values from -8 to 8
- factor: bfloat16 [2, 8192, 4, 512], P(None, 'rows', None, 'rhs'), may hold values from -0.125 to 0.125
- inverses: float32 [4, 512, 512], replicated, may hold values from -1 to 1, as said below
Outputs:
- state: float32 [2, 8192, 4096], P(None, 'rows', 'rhs')
Inputs may be any that keep to these rules, and one draw needn't show every extreme that they name: Each inverses[p] is unit lower triangular: ones on the diagonal, zeros above it.
All inputs are finite; a program needn't handle non-finite values.
Results may differ from a plain program's by a relative error of at most 0.003.
Values may be sent and summed in bfloat16 or wider, within the bound.
A program may use at most 128 MiB of HBM per device.

v0:
```python
import jax
import jax.numpy as jnp
from jax import lax
from jax.sharding import PartitionSpec as P


def from_root(value, axis, root):
    mine = lax.axis_index(axis) == root
    return lax.psum(jnp.where(mine, value, jnp.zeros_like(value)), axis)


def local(rhs, factor, inverses):
    count = lax.axis_size("rows")
    place = lax.axis_index("rows")
    cycles = rhs.shape[0]
    panels = inverses.shape[0]
    tile_ids = jnp.arange(cycles, dtype=jnp.int32) * count + place
    whole = lax.all_gather(factor, "rhs", axis=3, tiled=True)
    state = rhs
    for panel in range(panels):
        panel_cols = whole[:, :, panel, :]
        solved = jnp.dot(inverses[panel], state[0], precision=lax.Precision.HIGHEST)
        solved, sent = (solved, from_root(solved.astype(jnp.bfloat16), "rows", panel))
        first = jnp.where(place == panel, solved, state[0])
        state = jnp.concatenate([first[None], state[1:]], axis=0)
        delta = jnp.einsum("crk,kn->crn", panel_cols, sent, preferred_element_type=jnp.float32)
        keep = (tile_ids > panel)[:, None, None]
        state = state - jnp.where(keep, delta, jnp.float32(0.0))
    return state


def solution(mesh):
    return jax.shard_map(
        local,
        mesh=mesh,
        in_specs=(P(None, "rows", "rhs"), P(None, "rows", None, "rhs"), P()),
        out_specs=P(None, "rows", "rhs"),
        check_vma=False,
    )
```

profile of v0, /device:TPU:0, one launch (start us, length us, event | category | flops | bytes accessed | tf_op | source)
XLA Modules:
  0.0 596.7 jit_solution(13893594509365422396)
XLA Ops:
  7.4 10.9 %convert_select_fusion = (bf16[512,2048]{1,0:T(8,128)(2,1)}, f32[512,2048]{1,0:T(8,128)}) fusion(pred[]{:T(512)S(6)} %eq.19, f32[2,512,2048]{2,1,0:T(8,128)} %param.3, f32[4,512,512]{2,1,0:T(8,128)} %param.5), kind=kOutput, calls=%fused_computation.31 | convolution fusion | flops 6444548096 | bytes 11534337 | tf_op jit(solution)/shard_map/dot_general | solution.py:22
  18.3 0.0 all-gather.2.cloned.1.call-start
  18.4 1.6 copy.4
  20.1 4.7 slice.54
  24.8 7.3 %fusion.5 = f32[1,512,2048]{2,1,0:T(8,128)} fusion(f32[512,2048]{1,0:T(8,128)} %get-tuple-element.6, f32[2,512,2048]{2,1,0:T(8,128)} %param.3, pred[]{:T(512)S(6)} %eq.19), kind=kLoop, calls=%fused_computation.19 | loop fusion | flops 1048576 | bytes 12582913 | tf_op jit(solution)/shard_map/broadcast_in_dim | solution.py:25
  32.1 115.7 %all-reduce.5.cloned.1.call-done = bf16[512,2048]{1,0:T(8,128)(2,1)} async-done(((bf16[512,2048]{1,0:T(8,128)(2,1)}), bf16[512,2048]{1,0:T(8,128)(2,1)}) %all-reduce.5.cloned.1.call-update) | async-done | bytes 2097168 | tf_op jit(solution)/shard_map/psum | solution.py:9
  147.8 7.0 %maximum_subtract_fusion = f32[2,512,2048]{2,1,0:T(8,128)S(1)} fusion(f32[1,512,2048]{2,1,0:T(8,128)} %slice.54, f32[1,512,2048]{2,1,0:T(8,128)} %fusion.5, pred[2]{0:T(512)(128)(4,1)S(1)} %broadcast_compare_fusion.3, bf16[512,2048]{1,0:T(8,128)(2,1)} %all-reduce.5.cloned.1.call-done, bf16[2,512,4,512]{3,1,0,2:T(8,128)(2,1)} %all-gather.2.cloned.1.call-done), kind=kOutput, calls=%fused_computation | convolution fusion | flops 2153775104 | bytes 19922946 | tf_op jit(solution)/shard_map/crk,kn->crn/dot_general | solution.py:26
  154.9 10.8 %fusion.10 = (bf16[512,2048]{1,0:T(8,128)(2,1)}, f32[2048,512]{0,1:T(8,128)}) fusion(pred[]{:T(512)S(6)} %eq.18, f32[4,512,512]{2,1,0:T(8,128)} %param.5, f32[2,512,2048]{2,1,0:T(8,128)S(1)} %maximum_subtract_fusion), kind=kOutput, calls=%fused_computation.24 | convolution fusion | flops 6444548096 | bytes 11534337 | tf_op jit(solution)/shard_map/dot_general | solution.py:22
  165.7 0.2 all-reduce.9.cloned.1.call-start
  166.0 4.8 slice.70
  170.8 4.9 fusion.2
  175.7 115.9 %all-reduce.7.cloned.1.call-done = bf16[512,2048]{1,0:T(8,128)(2,1)} async-done(((bf16[512,2048]{1,0:T(8,128)(2,1)}), bf16[512,2048]{1,0:T(8,128)(2,1)}) %all-reduce.7.cloned.1.call-update) | async-done | bytes 2097168 | tf_op jit(solution)/shard_map/psum | solution.py:9
  291.6 7.0 %maximum_subtract_fusion.1 = f32[2,512,2048]{2,1,0:T(8,128)S(1)} fusion(f32[1,512,2048]{2,1,0:T(8,128)} %slice.70, f32[1,512,2048]{2,1,0:T(8,128)} %fusion.2, pred[2]{0:T(512)(128)(4,1)S(1)} %broadcast_compare_fusion.2, bf16[512,2048]{1,0:T(8,128)(2,1)} %all-reduce.7.cloned.1.call-done, bf16[2,512,4,512]{3,1,0,2:T(8,128)(2,1)} %all-gather.2.cloned.1.call-done), kind=kOutput, calls=%fused_computation.1 | convolution fusion | flops 2153775104 | bytes 19922946 | tf_op jit(solution)/shard_map/crk,kn->crn/dot_general | solution.py:26
  298.7 10.8 %fusion.11 = (bf16[512,2048]{1,0:T(8,128)(2,1)}, f32[2048,512]{0,1:T(8,128)}) fusion(pred[]{:T(512)S(6)} %eq.17, f32[4,512,512]{2,1,0:T(8,128)} %param.5, f32[2,512,2048]{2,1,0:T(8,128)S(1)} %maximum_subtract_fusion.1), kind=kOutput, calls=%fused_computation.25 | convolution fusion | flops 6444548096 | bytes 11534337 | tf_op jit(solution)/shard_map/dot_general | solution.py:22
  309.5 0.3 all-reduce.11.cloned.1.call-start
  309.8 4.8 slice.73
  314.6 4.9 fusion.1
  319.6 116.0 %all-reduce.9.cloned.1.call-done = bf16[512,2048]{1,0:T(8,128)(2,1)} async-done(((bf16[512,2048]{1,0:T(8,128)(2,1)}), bf16[512,2048]{1,0:T(8,128)(2,1)}) %all-reduce.9.cloned.1.call-update) | async-done | bytes 2097168 | tf_op jit(solution)/shard_map/psum | solution.py:9
  435.6 7.0 %maximum_subtract_fusion.2 = f32[2,512,2048]{2,1,0:T(8,128)S(1)} fusion(f32[1,512,2048]{2,1,0:T(8,128)} %slice.73, f32[1,512,2048]{2,1,0:T(8,128)} %fusion.1, pred[2]{0:T(512)(128)(4,1)S(1)} %broadcast_compare_fusion.1, bf16[512,2048]{1,0:T(8,128)(2,1)} %all-reduce.9.cloned.1.call-done, bf16[2,512,4,512]{3,1,0,2:T(8,128)(2,1)} %all-gather.2.cloned.1.call-done), kind=kOutput, calls=%fused_computation.2 | convolution fusion | flops 2153775104 | bytes 19922946 | tf_op jit(solution)/shard_map/crk,kn->crn/dot_general | solution.py:26
  442.6 10.8 %fusion.12 = (bf16[512,2048]{1,0:T(8,128)(2,1)}, f32[2048,512]{0,1:T(8,128)}) fusion(pred[]{:T(512)S(6)} %eq.16, f32[4,512,512]{2,1,0:T(8,128)} %param.5, f32[2,512,2048]{2,1,0:T(8,128)S(1)} %maximum_subtract_fusion.2), kind=kOutput, calls=%fused_computation.26 | convolution fusion | flops 6444548096 | bytes 11534337 | tf_op jit(solution)/shard_map/dot_general | solution.py:22
  453.5 4.8 slice.76
  458.3 5.0 fusion
  463.2 116.2 %all-reduce.11.cloned.1.call-done = bf16[512,2048]{1,0:T(8,128)(2,1)} async-done(((bf16[512,2048]{1,0:T(8,128)(2,1)}), bf16[512,2048]{1,0:T(8,128)(2,1)}) %all-reduce.11.cloned.1.call-update) | async-done | bytes 2097168 | tf_op jit(solution)/shard_map/psum | solution.py:9
  579.5 10.1 %maximum_subtract_fusion.3 = f32[2,512,2048]{2,1,0:T(8,128)} fusion(f32[1,512,2048]{2,1,0:T(8,128)} %slice.76, f32[1,512,2048]{2,1,0:T(8,128)} %fusion, pred[2]{0:T(512)(128)(4,1)S(1)} %broadcast_compare_fusion, bf16[512,2048]{1,0:T(8,128)(2,1)} %all-reduce.11.cloned.1.call-done, bf16[2,512,4,512]{3,1,0,2:T(8,128)(2,1)} %all-gather.2.cloned.1.call-done), kind=kOutput, calls=%fused_computation.3 | convolution fusion | flops 2153775104 | bytes 19922946 | tf_op jit(solution)/shard_map/crk,kn->crn/dot_general | solution.py:26
  (26 shorter events, 0.2 us)
Async XLA Ops:
  7.4 140.5 %all-reduce.5.cloned.1.call-start = ((), (), s32[]{:S(2)}) async-start(), calls=%async_computation | async-start | bytes 4194304 | tf_op jit(solution)/shard_map/psum | solution.py:9
  7.4 11.0 %copy-start.6 = (bf16[2,512,4,256]{3,2,1,0:T(4,128)(2,1)S(1)}, bf16[2,512,4,256]{3,2,1,0:T(4,128)(2,1)}, u32[]{:S(2)}) copy-start(bf16[2,512,4,256]{3,2,1,0:T(4,128)(2,1)} %param.4) | copy-start | bytes 6291460
  18.3 129.5 %all-gather.2.cloned.1.call-start = ((), (), s32[]{:S(2)}) async-start(), calls=%async_computation.1 | async-start | bytes 6291456 | tf_op jit(solution)/shard_map/all_gather | solution.py:18
  20.0 271.6 %all-reduce.7.cloned.1.call-start = ((), (), s32[]{:S(2)}) async-start(), calls=%async_computation.2 | async-start | bytes 4194304 | tf_op jit(solution)/shard_map/psum | solution.py:9
  154.8 10.8 %copy-start.3 = (f32[2,512,2048]{2,1,0:T(8,128)}, f32[2,512,2048]{2,1,0:T(8,128)S(1)}, u32[]{:S(2)}) copy-start(f32[2,512,2048]{2,1,0:T(8,128)S(1)} %maximum_subtract_fusion) | copy-start | bytes 25165828
  165.7 269.8 %all-reduce.9.cloned.1.call-start = ((), (), s32[]{:S(2)}) async-start(), calls=%async_computation.3 | async-start | bytes 4194304 | tf_op jit(solution)/shard_map/psum | solution.py:9
  166.0 4.8 copy-start
  298.6 10.8 %copy-start.4 = (f32[2,512,2048]{2,1,0:T(8,128)}, f32[2,512,2048]{2,1,0:T(8,128)S(1)}, u32[]{:S(2)}) copy-start(f32[2,512,2048]{2,1,0:T(8,128)S(1)} %maximum_subtract_fusion.1) | copy-start | bytes 25165828
  309.5 269.9 %all-reduce.11.cloned.1.call-start = ((), (), s32[]{:S(2)}) async-start(), calls=%async_computation.4 | async-start | bytes 4194304 | tf_op jit(solution)/shard_map/psum | solution.py:9
  309.8 4.8 copy-start.1
  442.6 10.8 %copy-start.5 = (f32[2,512,2048]{2,1,0:T(8,128)}, f32[2,512,2048]{2,1,0:T(8,128)S(1)}, u32[]{:S(2)}) copy-start(f32[2,512,2048]{2,1,0:T(8,128)S(1)} %maximum_subtract_fusion.2) | copy-start | bytes 25165828
  453.4 4.8 copy-start.2
Sparse Core Ops, SparseCore 0:
  18.5 129.3 all-reduce.4
  165.8 125.7 all-reduce.6
  309.6 125.8 all-reduce.8
  453.5 125.8 all-reduce.10
Sparse Core Ops, SparseCore 1:
  20.4 15.3 all-gather.1
where the time goes:
time: 597 us
  waiting for transfers between devices  464 us (78%)
  matrix products  74.5 us (12%)
  other arithmetic  22.2 us (4%)
  local copies, waits for them, and re-layouts  20.8 us (3%)
  between operations  14.7 us (2%)
    psum x4, waiting for transfers between devices, from_root(): return lax.psum(jnp.where(mine, value, jnp.zeros_like(value)), axis)  464 us
    dot_general x4, matrix products, local(): solved = jnp.dot(inverses[panel], state[0], precision=lax.Precision.HIGHEST)  43.4 us
    dot_general x4, matrix products, local(): jnp.einsum('crk,kn->crn', panel_cols, sent, preferred_element_type=jnp.fl...  31.1 us
    broadcast_in_dim x4, other arithmetic, local(): state = jnp.concatenate([first[None], state[1:]], axis=0)  22.2 us
    slice x4, local copies, waits for them, and re-layouts, local(): state = jnp.concatenate([first[None], state[1:]], axis=0)  19.1 us
  transfers between devices with their start and end apart: 5, of which 4 were waited for; matrix products, arithmetic and copies ran while one was open for 7% of the time, Pallas kernels for 0%

commit v1 on v0

v1 whole, which is shorter than its diff:
```python
import jax
import jax.numpy as jnp
from jax import lax
from jax.sharding import PartitionSpec as P


def local(rhs, factor, inverses):
    count = lax.axis_size("rows")
    place = lax.axis_index("rows")
    cycles, tile, width = rhs.shape
    panels = inverses.shape[0]
    bf16, f32 = jnp.bfloat16, jnp.float32
    tile_ids = jnp.arange(cycles, dtype=jnp.int32) * count + place

    pairs = [(t, p) for t in range(panels) for p in range(t)]
    blocks = jnp.stack([jnp.where(place == t, factor[0, :, p, :], jnp.zeros((), bf16)) for t, p in pairs])
    blocks = lax.all_gather(lax.psum(blocks, "rows"), "rhs", axis=2, tiled=True)
    block_of = {pair: blocks[i] for i, pair in enumerate(pairs)}

    pivots = lax.all_to_all(rhs[0], "rows", split_axis=1, concat_axis=0, tiled=True)
    sent = []
    for t in range(panels):
        pivot = pivots[t * tile:(t + 1) * tile]
        for p in range(t):
            pivot = pivot - jnp.dot(block_of[t, p], sent[p], preferred_element_type=f32)
        solved = jnp.dot(inverses[t], pivot, precision=lax.Precision.HIGHEST)
        sent.append(solved.astype(bf16))
    every = lax.all_gather(jnp.concatenate(sent, axis=0), "rows", axis=0)
    every = jnp.transpose(every, (1, 0, 2)).reshape(panels * tile, width)

    whole = lax.all_gather(factor, "rhs", axis=3, tiled=True)
    seen = tile_ids[:, None] > jnp.arange(panels, dtype=jnp.int32)[None, :]
    whole = jnp.where(seen[:, None, :, None], whole, jnp.zeros((), bf16))
    whole = whole.reshape(cycles, tile, panels * tile)
    state = rhs - jnp.einsum("crk,kn->crn", whole, every, preferred_element_type=f32)
    at = jnp.minimum(place, panels - 1) * tile
    mine = lax.dynamic_slice_in_dim(every, at, tile, axis=0).astype(f32)
    first = jnp.where(place < panels, mine, state[0])
    return jnp.concatenate([first[None], state[1:]], axis=0)


def solution(mesh):
    return jax.shard_map(
        local,
        mesh=mesh,
        in_specs=(P(None, "rows", "rhs"), P(None, "rows", None, "rhs"), P()),
        out_specs=P(None, "rows", "rhs"),
        check_vma=False,
    )
```

time: 597 us -> 416 us (0.70)
  waiting for transfers between devices: 464 us -> 293 us
  matrix products: 74.5 us -> 27.6 us
  local copies, waits for them, and re-layouts: 20.8 us -> 59 us
  other arithmetic: 22.2 us -> 13.7 us
  starting transfers between devices: 0.57 us -> 8.68 us
    psum x4 -> x1, waiting for transfers between devices: 464 us -> 179 us  [local(): blocks = lax.all_gather(lax.psum(blocks, 'rows'), 'rhs', axis=2, tiled=True)]
    all_gather x0 -> x2, waiting for transfers between devices: none -> 112 us  [the longest x1 102 us: local(): every = lax.all_gather(jnp.concatenate(sent, axis=0), 'rows', axis=0)]
    dot_general x8 -> x11, matrix products: 74.5 us -> 27.6 us  [the longest x1 12.6 us: local(): jnp.einsum('crk,kn->crn', whole, every, preferred_element_type=f32)]
    reshape x0 -> x3, local copies, waits for them, and re-layouts: none -> 30.5 us  [the longest x2 22.7 us: local(): every = jnp.transpose(every, (1, 0, 2)).reshape(panels * tile, width)]
    broadcast_in_dim x4 -> x1, other arithmetic: 22.2 us -> 2.5 us  [local(): return jnp.concatenate([first[None], state[1:]], axis=0)]
    slice x4 -> x3, local copies, waits for them, and re-layouts: 19.1 us -> 6.29 us  [the longest x1 4.7 us: local(): rhs[0]]
    transpose x0 -> x1, local copies, waits for them, and re-layouts: none -> 10.3 us  [local(): every = jnp.transpose(every, (1, 0, 2)).reshape(panels * tile, width)]
    all_to_all x0 -> x1, starting transfers between devices: none -> 8.52 us  [local(): lax.all_to_all(rhs[0], 'rows', split_axis=1, concat_axis=0, tiled=True)]
where the time goes in v1:
time: 416 us; the launch traced here: 415 us
  waiting for transfers between devices  293 us (70%)
  local copies, waits for them, and re-layouts  59 us (14%)
  matrix products  27.6 us (7%)
  other arithmetic  13.7 us (3%)
  between operations  13.3 us (3%)
  starting transfers between devices  8.68 us (2%)
    psum x1, waiting for transfers between devices, local(): blocks = lax.all_gather(lax.psum(blocks, 'rows'), 'rhs', axis=2, tiled=True)  179 us
    all_gather x1, waiting for transfers between devices, local(): every = lax.all_gather(jnp.concatenate(sent, axis=0), 'rows', axis=0)  102 us
    reshape x2, local copies, waits for them, and re-layouts, local(): every = jnp.transpose(every, (1, 0, 2)).reshape(panels * tile, width)  22.7 us
    dot_general x1, matrix products, local(): jnp.einsum('crk,kn->crn', whole, every, preferred_element_type=f32)  12.6 us
    transpose x1, local copies, waits for them, and re-layouts, local(): every = jnp.transpose(every, (1, 0, 2)).reshape(panels * tile, width)  10.3 us
    all_gather x1, waiting for transfers between devices, local(): blocks = lax.all_gather(lax.psum(blocks, 'rows'), 'rhs', axis=2, tiled=True)  9.09 us
    dot_general x6, matrix products, local(): pivot = pivot - jnp.dot(block_of[t, p], sent[p], preferred_element_type=f32)  8.53 us
    all_to_all x1, starting transfers between devices, local(): lax.all_to_all(rhs[0], 'rows', split_axis=1, concat_axis=0, tiled=True)  8.52 us
  transfers between devices with their start and end apart: 5, of which 4 were waited for; matrix products, arithmetic and copies ran while one was open for 7% of the time, Pallas kernels for 0%

profile of v1, /device:TPU:0, one launch (start us, length us, event | category | flops | bytes accessed | tf_op | source)
XLA Modules:
  0.0 415.1 jit_solution(7265404325880932777)
XLA Ops:
  6.5 4.7 %slice.76 = f32[1,512,2048]{2,1,0:T(8,128)} slice(f32[2,512,2048]{2,1,0:T(8,128)} %param.3), slice={[0:1], [0:512], [0:2048]} | slice | bytes 8388608 | tf_op jit(solution)/shard_map/slice | solution.py:20
  11.2 5.4 %copy.39 = f32[1,512,2048]{1,2,0:T(8,128)} copy(f32[1,512,2048]{2,1,0:T(8,128)} %slice.76) | data formatting | bytes 8388608
  16.6 5.3 %copy.28 = f32[512,16,128]{2,0,1:T(8,128)} copy(f32[512,16,128]{0,2,1:T(8,128)} %bitcast.93) | data formatting | bytes 8388608 | tf_op jit(solution)/shard_map/all_to_all | solution.py:20
  21.9 8.5 %all-to-all-start = ((f32[512,16,128]{2,0,1:T(8,128)}), f32[512,16,128]{2,0,1:T(8,128)}, u32[]{:S(2)}, u32[]{:S(2)}) async-start(f32[512,16,128]{2,0,1:T(8,128)} %copy.28), calls=%async_computation | async-start | bytes 8388608 | tf_op jit(solution)/shard_map/all_to_all | solution.py:20
  33.2 178.8 %all-reduce.2.cloned.1.call-done = bf16[6,512,256]{2,1,0:T(8,128)(2,1)} async-done(((bf16[6,512,256]{2,1,0:T(8,128)(2,1)}), bf16[6,512,256]{2,1,0:T(8,128)(2,1)}) %all-reduce.2.cloned.1.call-update) | async-done | bytes 1572880 | tf_op jit(solution)/shard_map/psum | solution.py:17
  212.8 2.3 convolution_convert_fusion.3
  215.1 9.1 %all-gather.5.cloned.1.call-done = bf16[6,512,512]{2,1,0:T(8,128)(2,1)} async-done(((bf16[6,512,256]{2,1,0:T(8,128)(2,1)}), bf16[6,512,512]{2,1,0:T(8,128)(2,1)}) %all-gather.5.cloned.1.call-update) | async-done | bytes 3145744 | tf_op jit(solution)/shard_map/all_gather | solution.py:17
  224.2 1.6 convolution_subtract_fusion.6
  225.8 1.4 convolution_subtract_fusion.5
  227.2 1.4 convolution_subtract_fusion.3
  228.6 2.2 convolution_convert_fusion.2
  230.8 1.3 convolution_subtract_fusion.4
  232.1 1.4 convolution_subtract_fusion.2
  234.6 1.4 convolution_subtract_fusion.1
  238.0 1.8 all-gather.7.cloned.1.call-done
  239.7 5.9 %broadcast_select_fusion = bf16[2,512,4,512]{3,2,1,0:T(4,128)(2,1)} fusion(bf16[2,512,4,512]{3,2,1,0:T(4,128)(2,1)} %all-gather.7.cloned.1.call-done, pred[2,4]{1,0:T(4,128)(4,1)S(1)} %iota_compare_fusion), kind=kLoop, calls=%fused_computation.5 | loop fusion | flops 2097152 | bytes 8388616 | tf_op jit(solution)/shard_map/jit(_where)/select_n | solution.py:33
  245.7 7.8 %reshape.118 = bf16[2,512,2048]{2,1,0:T(8,128)(2,1)} reshape(bf16[2,512,4,512]{3,2,1,0:T(4,128)(2,1)} %broadcast_select_fusion) | data formatting | bytes 8388608 | tf_op jit(solution)/shard_map/reshape | solution.py:34
  253.5 102.4 %all-gather.9.cloned.1.call-done = bf16[32768,128]{1,0:T(8,128)(2,1)} async-done(((bf16[2048,128]{1,0:T(8,128)(2,1)}), bf16[32768,128]{1,0:T(8,128)(2,1)}) %all-gather.9.cloned.1.call-update) | async-done | bytes 8388624 | tf_op jit(solution)/shard_map/all_gather | solution.py:28
  355.9 10.3 %copy.35 = bf16[2048,16,128]{2,1,0:T(8,128)(2,1)} copy(bf16[2048,16,128]{2,0,1:T(8,128)(2,1)} %bitcast.91) | data formatting | bytes 16777216 | tf_op jit(solution)/shard_map/transpose | solution.py:29
  366.2 13.3 %reshape.120 = bf16[2048,2048,1]{1,0,2:T(8,128)(2,1)} reshape(bf16[2048,16,128]{2,1,0:T(8,128)(2,1)} %copy.35) | data formatting | bytes 16777216 | tf_op jit(solution)/shard_map/reshape | solution.py:29
  379.6 9.3 %copy.55 = bf16[16,256,8,128]{3,2,0,1:T(8,128)(2,1)} copy(bf16[16,256,8,128]{3,2,1,0:T(8,128)(2,1)} %bitcast.92) | data formatting | bytes 16777216 | tf_op jit(solution)/shard_map/reshape | solution.py:29
  388.9 12.6 %convolution_subtract_fusion = f32[2,512,2048]{2,1,0:T(8,128)S(1)} fusion(f32[2,512,2048]{2,1,0:T(8,128)} %param.3, bf16[2,512,2048]{2,1,0:T(8,128)(2,1)S(1)} %copy-done.2, bf16[2048,2048,1]{1,0,2:T(8,128)(2,1)} %reshape.120), kind=kOutput, calls=%fused_computation.6 | convolution fusion | flops 8592031744 | bytes 29360128 | tf_op jit(solution)/shard_map/crk,kn->crn/dot_general | solution.py:35
  402.0 2.5 fusion.1
  404.5 4.0 pad_maximum_fusion
  (30 shorter events, 6.9 us)
Async XLA Ops:
  21.9 8.6 %copy-start = (bf16[2,512,4,256]{3,2,1,0:T(4,128)(2,1)S(1)}, bf16[2,512,4,256]{3,2,1,0:T(4,128)(2,1)}, u32[]{:S(2)}) copy-start(bf16[2,512,4,256]{3,2,1,0:T(4,128)(2,1)} %param.4) | copy-start | bytes 6291460
  21.9 190.9 %all-to-all-start = ((f32[512,16,128]{2,0,1:T(8,128)}), f32[512,16,128]{2,0,1:T(8,128)}, u32[]{:S(2)}, u32[]{:S(2)}) async-start(f32[512,16,128]{2,0,1:T(8,128)} %copy.28), calls=%async_computation | async-start | bytes 8388608 | tf_op jit(solution)/shard_map/all_to_all | solution.py:20
  30.5 181.6 %all-reduce.2.cloned.1.call-start = ((), (), s32[]{:S(2)}) async-start(), calls=%async_computation.1 | async-start | bytes 3145728 | tf_op jit(solution)/shard_map/psum | solution.py:17
  32.0 1.2 copy-start.3
  33.2 191.0 %all-gather.5.cloned.1.call-start = ((), (), s32[]{:S(2)}) async-start(), calls=%async_computation.2 | async-start | bytes 4718592 | tf_op jit(solution)/shard_map/all_gather | solution.py:17
  212.0 27.7 %all-gather.7.cloned.1.call-start = ((), (), s32[]{:S(2)}) async-start(), calls=%async_computation.3 | async-start | bytes 6291456 | tf_op jit(solution)/shard_map/all_gather | solution.py:31
  212.8 143.1 %all-gather.9.cloned.1.call-start = ((), (), s32[]{:S(2)}) async-start(), calls=%async_computation.4 | async-start | bytes 8912896 | tf_op jit(solution)/shard_map/all_gather | solution.py:28
  224.2 9.4 %copy-start.1 = (f32[4,512,512]{2,1,0:T(8,128)S(1)}, f32[4,512,512]{2,1,0:T(8,128)}, u32[]{:S(2)}) copy-start(f32[4,512,512]{2,1,0:T(8,128)} %param.5) | copy-start | bytes 12582916
  379.6 9.3 %copy-start.2 = (bf16[2,512,2048]{2,1,0:T(8,128)(2,1)S(1)}, bf16[2,512,2048]{2,1,0:T(8,128)(2,1)}, u32[]{:S(2)}) copy-start(bf16[2,512,2048]{2,1,0:T(8,128)(2,1)} %reshape.118) | copy-start | bytes 12582916
Sparse Core Ops, SparseCore 0:
  36.7 175.3 all-reduce.1
  213.6 10.5 all-gather.4
  225.7 13.9 all-gather.6
  242.4 113.5 all-gather.8
